TPU v7x, 128 devices: a whole 4x4x4 slice. The times are simulated.
128 devices in a mesh: teacher: 8 (over z_hi, y), student: 16 (over z_lo, x, core).
Axes of the slice: x: 4, y: 4, z: 4 (z_hi: 2, z_lo: 2; z = z_hi * 2 + z_lo), core: 2. Of those that a mesh axis runs over, the one named last changes fastest.
Arguments:
- teacher_in: bfloat16 [16384, 8192], P('student', 'teacher')
- teacher_attn: bfloat16 [16384, 4096], P('student', 'teacher'), may hold values from -6 to 6
- teacher_out_proj: bfloat16 [4096, 8192], P('student', 'teacher'), may hold values from -0.09375 to 0.09375
- teacher_gain: bfloat16 [8192], P('teacher'), may hold values from 0.099609375 to 1.8984375
- projection: bfloat16 [8192, 4096], P('teacher', 'student'), may hold values from -0.0625 to 0.0625
- student_in: bfloat16 [16384, 4096], P('student', 'teacher')
- student_attn: bfloat16 [16384, 2048], P('student', 'teacher'), may hold values from -6 to 6
- student_out_proj: bfloat16 [2048, 4096], P('student', 'teacher'), may hold values from -0.125 to 0.125
- student_gain: bfloat16 [4096], P('teacher'), may hold values from 0.099609375 to 1.8984375
- token_ids: int32 [16384], P('student'), may hold values from 0 to 128004, as said below
- row_order: int32 [16384], replicated, may hold values from 0 to 16383, as said below
Outputs:
- grad_weight: float32 [2048, 4096], P('student', 'teacher')
- grad_gain: float32 [4096], P('teacher')
Inputs may be any that keep to these rules, and one draw needn't show every extreme that they name: `token_ids`: within each sequence of 1024 consecutive rows the rows holding 128004 form the sequence's tail, after at least 256 other rows; no other row holds 128004. `row_order`: A permutation of the 16384 rows. For student block k and teacher block b (blocks of 1024 rows), the entries k * 1024 + b * 64 to k * 1024 + (b + 1) * 64 - 1 name rows of teacher block b.
All inputs are finite; a program needn't handle non-finite values.
Results may differ from a plain program's by a relative error of at most 0.02.
Values may be sent and summed in bfloat16 or wider, within the bound.
A program may use at most 128 MiB of HBM per device.

v0:
```python
import math
import jax
import jax.numpy as jnp
from jax import lax
from jax.sharding import PartitionSpec as P

DT = 8192
DS = 4096
PAD_ID = 128004
epsilon = 1e-05


def rows_first(arrays, axis, dims):
    turned = [jnp.moveaxis(a, dim, 0) for a, dim in zip(arrays, dims)]
    both = jnp.concatenate([t.reshape(len(t), -1) for t in turned], axis=1)
    result, at, outs = (lax.all_gather(both, axis, axis=0, tiled=True), 0, [])
    for t, dim in zip(turned, dims):
        section = result[:, at : at + t[0].size].reshape(-1, *t.shape[1:])
        outs.append(jnp.moveaxis(section, 0, dim))
        at += t[0].size
    return tuple(outs)


def sent_to_all(array, axis):
    peers = lax.axis_size(axis)
    return lax.all_to_all(
        jnp.broadcast_to(array[None], (peers, *array.shape)), axis, 0, 0, tiled=True
    )


def of_everyone(array, axis):
    everything = sent_to_all(array, axis)
    return jnp.sum(everything, axis=0)


def sent_together(arrays, axis, split_dim, concat_dim, along):
    columns = [a.reshape(*a.shape[:along], -1) for a in arrays]
    both = jnp.concatenate(columns, axis=along)
    result, at, outs = (
        lax.all_to_all(both, axis, split_axis=split_dim, concat_axis=concat_dim, tiled=True),
        0,
        [],
    )
    for a, column in zip(arrays, columns):
        section = result[..., at : at + column.shape[along]]
        outs.append(section.reshape(*section.shape[:along], *a.shape[along:]))
        at += column.shape[along]
    return tuple(outs)


def in_blocks(array, dim, peers):
    shape = array.shape
    parts = array.reshape(*shape[:dim], peers, shape[dim] // peers, *shape[dim + 1 :])
    return jnp.moveaxis(parts, dim, 0)


def sent_and_summed(array, axis, dim):
    peers = lax.axis_size(axis)
    parts = lax.all_to_all(in_blocks(array, dim, peers), axis, 0, 0, tiled=True)
    return jnp.sum(parts.astype(jnp.float32), axis=0)


def shards(
    teacher_in,
    teacher_attn,
    teacher_out_proj,
    teacher_gain,
    projection,
    student_in,
    student_attn,
    student_out_proj,
    student_gain,
    token_ids,
    row_order,
):
    student_count = lax.axis_size("student")
    teacher_count = lax.axis_size("teacher")
    row_count = teacher_in.shape[0]
    piece_rows = row_count // student_count
    student_index = lax.axis_index("student")
    attn_all = lax.all_gather(teacher_attn, "teacher", axis=1, tiled=True)
    out_full, proj_full = rows_first((teacher_out_proj, projection), "student", (0, 1))
    branch = jnp.dot(attn_all, out_full, preferred_element_type=jnp.float32)
    residual = teacher_in.astype(jnp.float32) + branch
    square_sum = of_everyone(jnp.sum(residual * residual, axis=1), "teacher")
    teacher_scale = lax.rsqrt(square_sum / DT + epsilon)
    hidden = (residual * teacher_scale[:, None] * teacher_gain.astype(jnp.float32)[None, :]).astype(
        jnp.bfloat16
    )
    proj_blocks = proj_full.reshape(
        proj_full.shape[0], teacher_count, proj_full.shape[1] // teacher_count
    )
    row_blocks = row_order.reshape(student_count, student_count, piece_rows)
    local_rows = (
        lax.dynamic_index_in_dim(row_blocks, student_index, 1, keepdims=False)
        - student_index * row_count
    )
    live_rows = jnp.where(token_ids != PAD_ID, 1.0, 0.0).astype(jnp.bfloat16)
    mask_send = jnp.take(live_rows, local_rows, axis=0)
    columns = proj_blocks
    summed = lax.psum_scatter(
        jnp.einsum("tf,fko->kto", hidden, columns, preferred_element_type=jnp.float32).astype(
            jnp.bfloat16
        ),
        "teacher",
        scatter_dimension=0,
        tiled=True,
    ).astype(jnp.float32)
    target_rows = summed[0].astype(jnp.bfloat16)
    moved, mask_got = sent_together(
        (jnp.take(target_rows, local_rows, axis=0), mask_send), "student", 0, 0, 2
    )
    target = moved.reshape(row_count, moved.shape[2])
    weight_mask = mask_got.reshape(row_count).astype(jnp.float32)
    attn_student = lax.all_gather(student_attn, "teacher", axis=1, tiled=True)
    columns = attn_student
    student_branch = jnp.dot(
        columns,
        lax.all_gather(student_out_proj, "student", axis=0, tiled=True),
        preferred_element_type=jnp.float32,
    )
    student_res = student_in.astype(jnp.float32) + student_branch
    student_square = of_everyone(jnp.sum(student_res * student_res, axis=1), "teacher")
    student_scale = lax.rsqrt(student_square / DS + epsilon)
    normed = student_res * student_scale[:, None]
    gain_values = student_gain.astype(jnp.float32)[None, :]
    distance = normed * gain_values - target.astype(jnp.float32)
    loss_weight = 1.0 / math.sqrt(row_count * student_count)
    grad_out = distance * (weight_mask * loss_weight)[:, None]
    gain_part = jnp.sum(grad_out * normed, axis=0)
    grad_norm = grad_out * gain_values
    inner_sum = of_everyone(jnp.sum(grad_norm * normed, axis=1), "teacher")
    grad_res = (student_scale[:, None] * (grad_norm - normed * (inner_sum / DS)[:, None])).astype(
        jnp.bfloat16
    )
    columns = attn_student
    grad_weight = sent_and_summed(
        lax.dot_general(
            columns, grad_res, (((0,), (0,)), ((), ())), preferred_element_type=jnp.float32
        ).astype(jnp.bfloat16),
        "student",
        0,
    )
    grad_gain = of_everyone(gain_part, "student")
    return (grad_weight, grad_gain)


def solution(mesh):
    placed = (
        P("student", "teacher"),
        P("student", "teacher"),
        P("student", "teacher"),
        P("teacher"),
        P("teacher", "student"),
        P("student", "teacher"),
        P("student", "teacher"),
        P("student", "teacher"),
        P("teacher"),
        P("student"),
        P(),
    )
    return jax.shard_map(
        shards,
        mesh=mesh,
        in_specs=placed,
        out_specs=(P("student", "teacher"), P("teacher")),
        check_vma=False,
    )
```

profile of v0, /device:TPU:3, one launch (start us, length us, event | category | flops | bytes accessed | tf_op | source)
XLA Modules:
  0.0 564.8 jit_solution(5684495137640013331)
XLA Ops:
  7.2 0.0 copy-start.3
  7.2 0.0 all-gather.11.cloned.1.call-start
  7.2 0.7 all-gather.11.cloned.1.call-update
  7.9 0.0 all-gather.9.cloned.1.call-start
  8.0 1.2 copy.60
  9.2 0.0 copy-start
  9.2 1.1 pad_maximum_fusion.1
  10.3 0.0 all-gather.9.cloned.1.call-update
  10.4 0.0 all-gather.7.cloned.1.call-start
  10.4 0.7 all-gather.7.cloned.1.call-update
  11.1 0.0 all-gather.5.cloned.1.call-start
  11.1 0.5 all-gather.5.cloned.1.call-update
  11.7 0.0 copy-start.6
  11.7 2.6 copy.62
  14.3 116.5 %all-gather.11.cloned.1.call-done = bf16[1024,4096]{1,0:T(8,128)(2,1)} async-done(((bf16[1024,512]{1,0:T(8,128)(2,1)}), bf16[1024,4096]{1,0:T(8,128)(2,1)}) %all-gather.11.cloned.1.call-update) | async-done | bytes 8388624 | tf_op jit(solution)/shard_map/all_gather | solution.py:81
  130.8 99.5 %all-gather.9.cloned.1.call-done = bf16[4096,2048]{0,1:T(8,128)(2,1)} async-done(((bf16[256,2048]{0,1:T(8,128)(2,1)}), bf16[4096,2048]{0,1:T(8,128)(2,1)}) %all-gather.9.cloned.1.call-update) | async-done | bytes 16777232 | tf_op jit(solution)/shard_map/all_gather | solution.py:16
  230.3 15.4 %multiply_reduce_fusion = (f32[1024]{0:T(1024)S(1)}, f32[1024,1024]{1,0:T(8,128)}) fusion(bf16[1024,1024]{0,1:T(8,128)(2,1)} %copy.62, bf16[1024,4096]{1,0:T(8,128)(2,1)} %all-gather.11.cloned.1.call-done, bf16[4096,2048]{0,1:T(8,128)(2,1)} %all-gather.9.cloned.1.call-done), kind=kOutput, calls=%fused_computation.9 | convolution fusion | flops 8594127872 | bytes 23072768 | tf_op jit(solution)/shard_map/dot_general | solution.py:83
  245.8 0.6 broadcast_in_dim.34
  246.4 6.3 %all-to-all-start.1 = ((f32[8,1,1024]{2,1,0:T(1,128)}), f32[8,1,1024]{2,1,0:T(1,128)S(1)}, u32[]{:S(2)}, u32[]{:S(2)}) async-start(f32[8,1,1024]{2,1,0:T(1,128)} %broadcast_in_dim.34), calls=%async_computation.1 | async-start | bytes 65536 | tf_op jit(solution)/shard_map/all_to_all | solution.py:26
  252.7 0.2 reduce-scatter.2.cloned.1.call-start
  252.9 7.8 %slice_bitcast_fusion = bf16[1024,4096]{1,0:T(8,128)(2,1)} fusion(bf16[4096,2048]{0,1:T(8,128)(2,1)} %all-gather.9.cloned.1.call-done), kind=kLoop, calls=%fused_computation.4 | loop fusion | bytes 16777216 | tf_op jit(solution)/shard_map/transpose | solution.py:19
  260.7 12.1 %copy.61 = bf16[1024,4096]{0,1:T(8,128)(2,1)} copy(bf16[1024,4096]{1,0:T(8,128)(2,1)} %slice_bitcast_fusion) | data formatting | bytes 16777216 | tf_op jit(solution)/shard_map/transpose | solution.py:19
  272.9 0.0 all-to-all-done.1
  272.9 15.4 %convert_bitcast_fusion = bf16[8,1024,512]{1,2,0:T(8,128)(2,1)} fusion(bf16[1024,8,512]{0,2,1:T(8,128)(2,1)} %bitcast.38, f32[1024,1024]{1,0:T(8,128)} %get-tuple-element.11, bf16[1024,1024]{0,1:T(8,128)(2,1)S(1)} %copy-done.1, f32[1024]{0:T(1024)S(1)} %convert_element_type.58, f32[1024]{0:T(1024)S(1)} %add_rsqrt_fusion), kind=kOutput, calls=%fused_computation.5 | convolution fusion | flops 8599371776 | bytes 23076864 | tf_op jit(solution)/shard_map/tf,fko->kto/dot_general | solution.py:102
  288.4 0.0 reduce-scatter.2.cloned.1.call-update
  288.4 0.8 copy-done.4
  289.2 0.1 reshape.115
  289.3 0.1 reshape.121
  289.4 0.0 copy-start.2
  289.4 6.8 %gather_fusion.1 = bf16[1024]{0:T(1024)(128)(2,1)S(1)} fusion(bf16[1024]{0:T(1024)(128)(2,1)S(1)} %select_convert_fusion, s32[1024]{0:T(1024)S(1)} %broadcast_clamp_fusion), kind=kCustom, calls=%fused_computation.1 | custom fusion | bytes 8192 | tf_op jit(solution)/shard_map/jit(_take)/gather | solution.py:99
  296.2 0.1 gather.12
  296.3 0.2 copy.66
  296.6 0.5 copy.58
  297.1 0.0 all-gather.7.cloned.1.call-done
  297.1 46.7 %all-gather.5.cloned.1.call-done = bf16[1024,2048]{1,0:T(8,128)(2,1)} async-done(((bf16[1024,256]{1,0:T(8,128)(2,1)}), bf16[1024,2048]{1,0:T(8,128)(2,1)}) %all-gather.5.cloned.1.call-update) | async-done | bytes 4194320 | tf_op jit(solution)/shard_map/all_gather | solution.py:115
  343.9 6.6 %multiply_reduce_fusion.3 = (f32[1024]{0:T(1024)S(1)}, f32[1024,512]{0,1:T(8,128)}) fusion(bf16[1024,2048]{1,0:T(8,128)(2,1)} %all-gather.5.cloned.1.call-done, bf16[2048,512]{1,0:T(8,128)(2,1)} %all-gather.7.cloned.1.call-done, bf16[1024,512]{0,1:T(8,128)(2,1)S(1)} %copy.58), kind=kOutput, calls=%fused_computation.19 | convolution fusion | flops 2149579776 | bytes 9441280 | tf_op jit(solution)/shard_map/dot_general | solution.py:117
  350.5 0.6 broadcast_in_dim.32
  351.1 3.4 all-to-all-start
  354.5 107.1 %reduce-scatter.2.cloned.1.call-done = bf16[1,1024,512]{1,2,0:T(8,128)(2,1)} async-done(((bf16[8,1024,512]{1,2,0:T(8,128)(2,1)}), bf16[1,1024,512]{1,2,0:T(8,128)(2,1)}) %reduce-scatter.2.cloned.1.call-update) | async-done | bytes 1048592 | tf_op jit(solution)/shard_map/reduce_scatter | solution.py:101
  461.6 1.5 copy.65
  463.1 4.0 gather_fusion
  467.0 0.2 broadcast_select_fusion
  467.2 0.0 copy-start.7
  467.3 1.2 pad_maximum_fusion
  468.4 0.0 all-to-all-done
  468.4 5.9 %all-to-all-start.2 = ((bf16[16,64,513]{2,1,0:T(8,128)(2,1)}), bf16[16,64,513]{2,1,0:T(8,128)(2,1)S(1)}, u32[]{:S(2)}, u32[]{:S(2)}) async-start(bf16[16,64,513]{2,1,0:T(8,128)(2,1)} %pad_maximum_fusion), calls=%async_computation.3 | async-start | bytes 2621440 | tf_op jit(solution)/shard_map/all_to_all | solution.py:40
  474.5 16.8 %all-to-all-done.2 = bf16[16,64,513]{2,1,0:T(8,128)(2,1)S(1)} async-done(((bf16[16,64,513]{2,1,0:T(8,128)(2,1)}), bf16[16,64,513]{2,1,0:T(8,128)(2,1)S(1)}, u32[]{:S(2)}, u32[]{:S(2)}) %all-to-all-start.2) | async-done | bytes 1050656 | tf_op jit(solution)/shard_map/all_to_all | solution.py:40
  491.2 0.1 slice.22
  491.3 1.7 bitcast_convert_fusion
  493.0 1.9 copy.67
  494.9 0.2 multiply_reduce_fusion.4
  495.2 0.1 mul.101
  495.2 2.4 multiply_reduce_fusion.1
  497.6 10.2 %all_to_all.34 = f32[8,1,1024]{2,1,0:T(1,128)S(1)} all-to-all(f32[8,1,1024]{2,1,0:T(1,128)S(1)} %broadcast_in_dim.62), channel_id=1, replica_groups=mesh['teacher'=8,'student'=16] {'teacher'}, dimensions={0} | all-to-all | bytes 65536 | tf_op jit(solution)/shard_map/all_to_all | solution.py:26
  507.8 0.6 broadcast_in_dim.63
  508.4 7.2 %all-to-all-start.5 = ((f32[16,1,512]{2,1,0:T(1,128)}), f32[16,1,512]{2,1,0:T(1,128)S(1)}, u32[]{:S(2)}, u32[]{:S(2)}) async-start(f32[16,1,512]{2,1,0:T(1,128)} %broadcast_in_dim.63), calls=%async_computation.6 | async-start | bytes 65536 | tf_op jit(solution)/shard_map/all_to_all | solution.py:26
  515.7 5.4 fusion.6
  521.1 1.9 copy.82
  522.9 0.0 all-to-all-done.5
  523.0 5.8 %all-to-all-start.4 = ((bf16[16,128,512]{1,2,0:T(8,128)(2,1)}), bf16[16,128,512]{1,2,0:T(8,128)(2,1)S(1)}, u32[]{:S(2)}, u32[]{:S(2)}) async-start(bf16[16,128,512]{1,2,0:T(8,128)(2,1)} %bitcast.37), calls=%async_computation.5 | async-start | bytes 4194304 | tf_op jit(solution)/shard_map/all_to_all | solution.py:59
  528.8 0.6 reduce_sum.89
  529.4 27.7 %all-to-all-done.4 = bf16[16,128,512]{1,2,0:T(8,128)(2,1)S(1)} async-done(((bf16[16,128,512]{1,2,0:T(8,128)(2,1)}), bf16[16,128,512]{1,2,0:T(8,128)(2,1)S(1)}, u32[]{:S(2)}, u32[]{:S(2)}) %all-to-all-start.4) | async-done | bytes 2097184 | tf_op jit(solution)/shard_map/all_to_all | solution.py:59
  557.1 0.3 convert_reduce_fusion
  557.4 0.8 copy.72
  (25 shorter events, 0.2 us)
Async XLA Ops:
  7.2 2.1 copy-start.3
  7.2 123.6 %all-gather.11.cloned.1.call-start = ((), (), s32[]{:S(2)}) async-start(), calls=%async_computation.10 | async-start | bytes 9437184 | tf_op jit(solution)/shard_map/all_gather | solution.py:81
  7.9 222.4 %all-gather.9.cloned.1.call-start = ((), (), s32[]{:S(2)}) async-start(), calls=%async_computation.9 | async-start | bytes 17825792 | tf_op jit(solution)/shard_map/all_gather | solution.py:16
  9.2 2.5 copy-start
  10.4 286.8 %all-gather.7.cloned.1.call-start = ((), (), s32[]{:S(2)}) async-start(), calls=%async_computation.8 | async-start | bytes 2228224 | tf_op jit(solution)/shard_map/all_gather | solution.py:119
  11.1 332.8 %all-gather.5.cloned.1.call-start = ((), (), s32[]{:S(2)}) async-start(), calls=%async_computation.7 | async-start | bytes 4718592 | tf_op jit(solution)/shard_map/all_gather | solution.py:115
  11.7 2.6 copy-start.6
  246.4 26.5 %all-to-all-start.1 = ((f32[8,1,1024]{2,1,0:T(1,128)}), f32[8,1,1024]{2,1,0:T(1,128)S(1)}, u32[]{:S(2)}, u32[]{:S(2)}) async-start(f32[8,1,1024]{2,1,0:T(1,128)} %broadcast_in_dim.34), calls=%async_computation.1 | async-start | bytes 65536 | tf_op jit(solution)/shard_map/all_to_all | solution.py:26
  252.7 208.9 %reduce-scatter.2.cloned.1.call-start = ((), (), s32[]{:S(2)}) async-start(), calls=%async_computation.11 | async-start | bytes 9437184 | tf_op jit(solution)/shard_map/reduce_scatter | solution.py:101
  260.7 12.2 %copy-start.1 = (bf16[1024,1024]{0,1:T(8,128)(2,1)S(1)}, bf16[1024,1024]{0,1:T(8,128)(2,1)}, u32[]{:S(2)}) copy-start(bf16[1024,1024]{0,1:T(8,128)(2,1)} %copy.62) | copy-start | bytes 6291460
  288.4 0.8 copy-start.4
  288.4 1.0 copy-start.5
  289.4 7.1 %copy-start.2 = (bf16[1024,512]{1,0:T(8,128)(2,1)S(1)}, bf16[1024,512]{1,0:T(8,128)(2,1)}, u32[]{:S(2)}) copy-start(bf16[1024,512]{1,0:T(8,128)(2,1)} %param.16) | copy-start | bytes 3145732
  351.1 117.4 %all-to-all-start = ((f32[8,1,1024]{2,1,0:T(1,128)}), f32[8,1,1024]{2,1,0:T(1,128)S(1)}, u32[]{:S(2)}, u32[]{:S(2)}) async-start(f32[8,1,1024]{2,1,0:T(1,128)} %broadcast_in_dim.32), calls=%async_computation | async-start | bytes 65536 | tf_op jit(solution)/shard_map/all_to_all | solution.py:26
  467.2 7.2 %copy-start.7 = (bf16[512]{0:T(512)(128)(2,1)S(1)}, bf16[512]{0:T(512)(128)(2,1)}, u32[]{:S(2)}) copy-start(bf16[512]{0:T(512)(128)(2,1)} %param.19) | copy-start | bytes 3076
  468.4 22.8 %all-to-all-start.2 = ((bf16[16,64,513]{2,1,0:T(8,128)(2,1)}), bf16[16,64,513]{2,1,0:T(8,128)(2,1)S(1)}, u32[]{:S(2)}, u32[]{:S(2)}) async-start(bf16[16,64,513]{2,1,0:T(8,128)(2,1)} %pad_maximum_fusion), calls=%async_computation.3 | async-start | bytes 2621440 | tf_op jit(solution)/shard_map/all_to_all | solution.py:40
  508.4 14.5 %all-to-all-start.5 = ((f32[16,1,512]{2,1,0:T(1,128)}), f32[16,1,512]{2,1,0:T(1,128)S(1)}, u32[]{:S(2)}, u32[]{:S(2)}) async-start(f32[16,1,512]{2,1,0:T(1,128)} %broadcast_in_dim.63), calls=%async_computation.6 | async-start | bytes 65536 | tf_op jit(solution)/shard_map/all_to_all | solution.py:26
  523.0 34.1 %all-to-all-start.4 = ((bf16[16,128,512]{1,2,0:T(8,128)(2,1)}), bf16[16,128,512]{1,2,0:T(8,128)(2,1)S(1)}, u32[]{:S(2)}, u32[]{:S(2)}) async-start(bf16[16,128,512]{1,2,0:T(8,128)(2,1)} %bitcast.37), calls=%async_computation.5 | async-start | bytes 4194304 | tf_op jit(solution)/shard_map/all_to_all | solution.py:59
Sparse Core Ops, SparseCore 0:
  10.2 120.5 all-gather.10
  132.4 97.8 all-gather.8
  232.0 33.8 all-gather.6
  267.9 75.8 all-gather.4
  347.6 113.9 reduce-scatter.1
where the time goes:
time: 566 us; the launch traced here: 565 us
  waiting for transfers between devices  416 us (73%)
  local copies, waits for them, and re-layouts  44.6 us (8%)
  matrix products  42.8 us (8%)
  starting transfers between devices  29.1 us (5%)
  between operations  14 us (2%)
  blocking collectives  10.2 us (2%)
  other arithmetic  7.84 us (1%)
    all_gather x1, waiting for transfers between devices, shards(): attn_all = lax.all_gather(teacher_attn, 'teacher', axis=1, tiled=True)  117 us
    reduce_scatter x1, waiting for transfers between devices, shards(): lax.psum_scatter(jnp.einsum('tf,fko->kto', hidden, columns, preferred_ele...  107 us
    all_gather x1, waiting for transfers between devices, rows_first(): result, at, outs = (lax.all_gather(both, axis, axis=0, tiled=True), 0, [])  99.5 us
    all_gather x1, waiting for transfers between devices, shards(): attn_student = lax.all_gather(student_attn, 'teacher', axis=1, tiled=True)  46.7 us
    all_to_all x1, waiting for transfers between devices, sent_and_summed(): parts = lax.all_to_all(in_blocks(array, dim, peers), axis, 0, 0, tiled=True)  27.7 us
    transpose x2, local copies, waits for them, and re-layouts, rows_first(): outs.append(jnp.moveaxis(section, 0, dim))  20 us
    all_to_all x3, starting transfers between devices, sent_to_all(): lax.all_to_all(jnp.broadcast_to(array[None], (peers, *array.shape)), axis...  17 us
    all_to_all x1, waiting for transfers between devices, sent_together(): lax.all_to_all(both, axis, split_axis=split_dim, concat_axis=concat_dim,...  16.8 us
  transfers between devices with their start and end apart: 10, of which 6 were waited for; matrix products, arithmetic and copies ran while one was open for 15% of the time, Pallas kernels for 0%

commit v1 on v0

--- a/solution.py
+++ b/solution.py
@@ -112,7 +112,7 @@
     )
     target = moved.reshape(row_count, moved.shape[2])
     weight_mask = mask_got.reshape(row_count).astype(jnp.float32)
-    attn_student = lax.all_gather(student_attn, "teacher", axis=1, tiled=True)
+    attn_student = jnp.concatenate(lax.all_gather(student_attn, "teacher"), axis=1)
     columns = attn_student
     student_branch = jnp.dot(
         columns,

time: 566 us -> 560 us (0.989)
  waiting for transfers between devices: 416 us -> 401 us
  local copies, waits for them, and re-layouts: 44.6 us -> 50.7 us
    all_gather x1, waiting for transfers between devices: 46.7 us -> 6.93 us  [shards(): lax.all_gather(student_attn, 'teacher')]
    all_gather x1, waiting for transfers between devices: 0.02 us -> 27.4 us  [shards(): lax.all_gather(student_out_proj, 'student', axis=0, tiled=True)]
    reshape x0 -> x1, local copies, waits for them, and re-layouts: none -> 6.51 us  [shards(): jnp.concatenate(lax.all_gather(student_attn, 'teacher'), axis=1)]
  transfers between devices with their start and end apart: 10 -> 10, of which waited for: 6 -> 7; matrix products, arithmetic and copies ran while one was open for 15% -> 17% of each run, Pallas kernels for 0% -> 0%
where the time goes in v1:
time: 560 us; the launch traced here: 559 us
  waiting for transfers between devices  401 us (72%)
  local copies, waits for them, and re-layouts  50.7 us (9%)
  matrix products  42.8 us (8%)
  starting transfers between devices  32 us (6%)
  between operations  14 us (2%)
  blocking collectives  10.2 us (2%)
  other arithmetic  7.84 us (1%)
    all_gather x1, waiting for transfers between devices, shards(): attn_all = lax.all_gather(teacher_attn, 'teacher', axis=1, tiled=True)  117 us
    reduce_scatter x1, waiting for transfers between devices, shards(): lax.psum_scatter(jnp.einsum('tf,fko->kto', hidden, columns, preferred_ele...  105 us
    all_gather x1, waiting for transfers between devices, rows_first(): result, at, outs = (lax.all_gather(both, axis, axis=0, tiled=True), 0, [])  99.5 us
    all_to_all x1, waiting for transfers between devices, sent_and_summed(): parts = lax.all_to_all(in_blocks(array, dim, peers), axis, 0, 0, tiled=True)  27.7 us
    all_gather x1, waiting for transfers between devices, shards(): lax.all_gather(student_out_proj, 'student', axis=0, tiled=True)  27.4 us
    all_to_all x3, starting transfers between devices, sent_to_all(): lax.all_to_all(jnp.broadcast_to(array[None], (peers, *array.shape)), axis...  19.9 us
    transpose x2, local copies, waits for them, and re-layouts, rows_first(): outs.append(jnp.moveaxis(section, 0, dim))  19.6 us
    all_to_all x1, waiting for transfers between devices, sent_together(): lax.all_to_all(both, axis, split_axis=split_dim, concat_axis=concat_dim,...  16.8 us
  transfers between devices with their start and end apart: 10, of which 7 were waited for; matrix products, arithmetic and copies ran while one was open for 17% of the time, Pallas kernels for 0%

profile of v1, /device:TPU:3, one launch (start us, length us, event | category | flops | bytes accessed | tf_op | source)
XLA Modules:
  0.0 558.9 jit_solution(8868351362170763385)
XLA Ops:
  7.2 0.0 all-gather.10.cloned.1.call-start
  7.2 0.7 all-gather.10.cloned.1.call-update
  7.9 0.0 all-gather.8.cloned.1.call-start
  8.0 1.2 copy.64
  9.2 0.0 copy-start
  9.2 1.1 pad_maximum_fusion.1
  10.3 0.0 all-gather.8.cloned.1.call-update
  10.4 0.0 all-gather.12.cloned.1.call-start
  10.4 0.7 all-gather.12.cloned.1.call-update
  11.1 0.0 all-gather.6.cloned.1.call-start
  11.1 0.5 all-gather.6.cloned.1.call-update
  11.7 0.0 copy-start.6
  11.7 2.6 copy.66
  14.3 116.5 %all-gather.10.cloned.1.call-done = bf16[1024,4096]{1,0:T(8,128)(2,1)} async-done(((bf16[1024,512]{1,0:T(8,128)(2,1)}), bf16[1024,4096]{1,0:T(8,128)(2,1)}) %all-gather.10.cloned.1.call-update) | async-done | bytes 8388624 | tf_op jit(solution)/shard_map/all_gather | solution.py:81
  130.8 99.5 %all-gather.8.cloned.1.call-done = bf16[4096,2048]{0,1:T(8,128)(2,1)} async-done(((bf16[256,2048]{0,1:T(8,128)(2,1)}), bf16[4096,2048]{0,1:T(8,128)(2,1)}) %all-gather.8.cloned.1.call-update) | async-done | bytes 16777232 | tf_op jit(solution)/shard_map/all_gather | solution.py:16
  230.3 15.4 %multiply_reduce_fusion = (f32[1024]{0:T(1024)S(1)}, f32[1024,1024]{1,0:T(8,128)}) fusion(bf16[1024,1024]{0,1:T(8,128)(2,1)} %copy.66, bf16[1024,4096]{1,0:T(8,128)(2,1)} %all-gather.10.cloned.1.call-done, bf16[4096,2048]{0,1:T(8,128)(2,1)} %all-gather.8.cloned.1.call-done), kind=kOutput, calls=%fused_computation.9 | convolution fusion | flops 8594127872 | bytes 23072768 | tf_op jit(solution)/shard_map/dot_general | solution.py:83
  245.8 0.6 broadcast_in_dim.34
  246.4 6.3 %all-to-all-start.1 = ((f32[8,1,1024]{2,1,0:T(1,128)}), f32[8,1,1024]{2,1,0:T(1,128)S(1)}, u32[]{:S(2)}, u32[]{:S(2)}) async-start(f32[8,1,1024]{2,1,0:T(1,128)} %broadcast_in_dim.34), calls=%async_computation.1 | async-start | bytes 65536 | tf_op jit(solution)/shard_map/all_to_all | solution.py:26
  252.7 0.2 reduce-scatter.2.cloned.1.call-start
  252.9 7.8 %slice_bitcast_fusion = bf16[1024,4096]{1,0:T(8,128)(2,1)} fusion(bf16[4096,2048]{0,1:T(8,128)(2,1)} %all-gather.8.cloned.1.call-done), kind=kLoop, calls=%fused_computation.4 | loop fusion | bytes 16777216 | tf_op jit(solution)/shard_map/transpose | solution.py:19
  260.7 11.8 %copy.65 = bf16[1024,4096]{0,1:T(8,128)(2,1)} copy(bf16[1024,4096]{1,0:T(8,128)(2,1)} %slice_bitcast_fusion) | data formatting | bytes 16777216 | tf_op jit(solution)/shard_map/transpose | solution.py:19
  272.5 0.0 all-to-all-done.1
  272.6 15.4 %convert_bitcast_fusion = bf16[8,1024,512]{1,2,0:T(8,128)(2,1)} fusion(bf16[1024,8,512]{0,2,1:T(8,128)(2,1)} %bitcast.42, f32[1024,1024]{1,0:T(8,128)} %get-tuple-element.11, bf16[1024,1024]{0,1:T(8,128)(2,1)S(1)} %copy-done.1, f32[1024]{0:T(1024)S(1)} %convert_element_type.58, f32[1024]{0:T(1024)S(1)} %add_rsqrt_fusion), kind=kOutput, calls=%fused_computation.5 | convolution fusion | flops 8599371776 | bytes 23076864 | tf_op jit(solution)/shard_map/tf,fko->kto/dot_general | solution.py:102
  288.0 0.0 reduce-scatter.2.cloned.1.call-update
  288.0 0.8 copy-done.4
  288.8 0.1 reshape.123
  289.0 0.1 reshape.129
  289.1 0.0 copy-start.2
  289.1 6.8 %gather_fusion.1 = bf16[1024]{0:T(1024)(128)(2,1)S(1)} fusion(bf16[1024]{0:T(1024)(128)(2,1)S(1)} %select_convert_fusion, s32[1024]{0:T(1024)S(1)} %broadcast_clamp_fusion), kind=kCustom, calls=%fused_computation.1 | custom fusion | bytes 8192 | tf_op jit(solution)/shard_map/jit(_take)/gather | solution.py:99
  295.9 0.1 gather.12
  296.0 0.2 copy.70
  296.2 0.5 copy.61
  296.8 6.9 %all-gather.12.cloned.1.call-done = bf16[8192,256]{1,0:T(8,128)(2,1)} async-done(((bf16[1024,256]{1,0:T(8,128)(2,1)}), bf16[8192,256]{1,0:T(8,128)(2,1)}) %all-gather.12.cloned.1.call-update) | async-done | bytes 4194320 | tf_op jit(solution)/shard_map/all_gather | solution.py:115
  303.7 6.5 %copy.62 = bf16[1024,8,256]{0,2,1:T(8,128)(2,1)} copy(bf16[1024,8,256]{2,0,1:T(8,128)(2,1)} %bitcast.43) | data formatting | bytes 8388608 | tf_op jit(solution)/shard_map/reshape | solution.py:115
  310.2 27.4 %all-gather.6.cloned.1.call-done = bf16[2048,512]{1,0:T(8,128)(2,1)} async-done(((bf16[128,512]{1,0:T(8,128)(2,1)}), bf16[2048,512]{1,0:T(8,128)(2,1)}) %all-gather.6.cloned.1.call-update) | async-done | bytes 2097168 | tf_op jit(solution)/shard_map/all_gather | solution.py:119
  337.6 6.6 %multiply_reduce_fusion.3 = (f32[1024]{0:T(1024)S(1)}, f32[1024,512]{0,1:T(8,128)}) fusion(bf16[1024,2048]{0,1:T(8,128)(2,1)} %bitcast.44, bf16[2048,512]{1,0:T(8,128)(2,1)} %all-gather.6.cloned.1.call-done, bf16[1024,512]{0,1:T(8,128)(2,1)S(1)} %copy.61), kind=kOutput, calls=%fused_computation.19 | convolution fusion | flops 2149579776 | bytes 9441280 | tf_op jit(solution)/shard_map/dot_general | solution.py:117
  344.1 0.6 broadcast_in_dim.32
  344.8 6.1 %all-to-all-start = ((f32[8,1,1024]{2,1,0:T(1,128)}), f32[8,1,1024]{2,1,0:T(1,128)S(1)}, u32[]{:S(2)}, u32[]{:S(2)}) async-start(f32[8,1,1024]{2,1,0:T(1,128)} %broadcast_in_dim.32), calls=%async_computation | async-start | bytes 65536 | tf_op jit(solution)/shard_map/all_to_all | solution.py:26
  350.9 104.5 %reduce-scatter.2.cloned.1.call-done = bf16[1,1024,512]{1,2,0:T(8,128)(2,1)} async-done(((bf16[8,1024,512]{1,2,0:T(8,128)(2,1)}), bf16[1,1024,512]{1,2,0:T(8,128)(2,1)}) %reduce-scatter.2.cloned.1.call-update) | async-done | bytes 1048592 | tf_op jit(solution)/shard_map/reduce_scatter | solution.py:101
  455.4 1.5 copy.69
  456.9 4.0 gather_fusion
  460.9 0.2 broadcast_select_fusion
  461.1 0.0 copy-start.7
  461.1 1.2 pad_maximum_fusion
  462.3 0.0 all-to-all-done
  462.3 6.0 %all-to-all-start.2 = ((bf16[16,64,513]{2,1,0:T(8,128)(2,1)}), bf16[16,64,513]{2,1,0:T(8,128)(2,1)S(1)}, u32[]{:S(2)}, u32[]{:S(2)}) async-start(bf16[16,64,513]{2,1,0:T(8,128)(2,1)} %pad_maximum_fusion), calls=%async_computation.3 | async-start | bytes 2621440 | tf_op jit(solution)/shard_map/all_to_all | solution.py:40
  468.4 16.8 %all-to-all-done.2 = bf16[16,64,513]{2,1,0:T(8,128)(2,1)S(1)} async-done(((bf16[16,64,513]{2,1,0:T(8,128)(2,1)}), bf16[16,64,513]{2,1,0:T(8,128)(2,1)S(1)}, u32[]{:S(2)}, u32[]{:S(2)}) %all-to-all-start.2) | async-done | bytes 1050656 | tf_op jit(solution)/shard_map/all_to_all | solution.py:40
  485.1 0.1 slice.22
  485.2 1.7 bitcast_convert_fusion
  486.9 1.9 copy.71
  488.8 0.2 multiply_reduce_fusion.4
  489.1 0.1 mul.101
  489.1 2.4 multiply_reduce_fusion.1
  491.5 10.2 %all_to_all.34 = f32[8,1,1024]{2,1,0:T(1,128)S(1)} all-to-all(f32[8,1,1024]{2,1,0:T(1,128)S(1)} %broadcast_in_dim.62), channel_id=1, replica_groups=mesh['teacher'=8,'student'=16] {'teacher'}, dimensions={0} | all-to-all | bytes 65536 | tf_op jit(solution)/shard_map/all_to_all | solution.py:26
  501.7 0.6 broadcast_in_dim.63
  502.4 7.5 %all-to-all-start.5 = ((f32[16,1,512]{2,1,0:T(1,128)}), f32[16,1,512]{2,1,0:T(1,128)S(1)}, u32[]{:S(2)}, u32[]{:S(2)}) async-start(f32[16,1,512]{2,1,0:T(1,128)} %broadcast_in_dim.63), calls=%async_computation.6 | async-start | bytes 65536 | tf_op jit(solution)/shard_map/all_to_all | solution.py:26
  509.9 5.4 fusion.6
  515.2 1.9 copy.86
  517.1 0.0 all-to-all-done.5
  517.1 5.8 %all-to-all-start.4 = ((bf16[16,128,512]{1,2,0:T(8,128)(2,1)}), bf16[16,128,512]{1,2,0:T(8,128)(2,1)S(1)}, u32[]{:S(2)}, u32[]{:S(2)}) async-start(bf16[16,128,512]{1,2,0:T(8,128)(2,1)} %bitcast.41), calls=%async_computation.5 | async-start | bytes 4194304 | tf_op jit(solution)/shard_map/all_to_all | solution.py:59
  522.9 0.6 reduce_sum.89
  523.5 27.7 %all-to-all-done.4 = bf16[16,128,512]{1,2,0:T(8,128)(2,1)S(1)} async-done(((bf16[16,128,512]{1,2,0:T(8,128)(2,1)}), bf16[16,128,512]{1,2,0:T(8,128)(2,1)S(1)}, u32[]{:S(2)}, u32[]{:S(2)}) %all-to-all-start.4) | async-done | bytes 2097184 | tf_op jit(solution)/shard_map/all_to_all | solution.py:59
  551.2 0.3 convert_reduce_fusion
  551.5 0.8 copy.76
  (26 shorter events, 0.2 us)
Async XLA Ops:
  7.2 2.1 copy-start.3
  7.2 123.6 %all-gather.10.cloned.1.call-start = ((), (), s32[]{:S(2)}) async-start(), calls=%async_computation.9 | async-start | bytes 9437184 | tf_op jit(solution)/shard_map/all_gather | solution.py:81
  7.9 222.4 %all-gather.8.cloned.1.call-start = ((), (), s32[]{:S(2)}) async-start(), calls=%async_computation.8 | async-start | bytes 17825792 | tf_op jit(solution)/shard_map/all_gather | solution.py:16
  9.2 2.5 copy-start
  10.4 293.3 %all-gather.12.cloned.1.call-start = ((), (), s32[]{:S(2)}) async-start(), calls=%async_computation.11 | async-start | bytes 4718592 | tf_op jit(solution)/shard_map/all_gather | solution.py:115
  11.1 326.5 %all-gather.6.cloned.1.call-start = ((), (), s32[]{:S(2)}) async-start(), calls=%async_computation.7 | async-start | bytes 2228224 | tf_op jit(solution)/shard_map/all_gather | solution.py:119
  11.7 2.6 copy-start.6
  246.4 26.1 %all-to-all-start.1 = ((f32[8,1,1024]{2,1,0:T(1,128)}), f32[8,1,1024]{2,1,0:T(1,128)S(1)}, u32[]{:S(2)}, u32[]{:S(2)}) async-start(f32[8,1,1024]{2,1,0:T(1,128)} %broadcast_in_dim.34), calls=%async_computation.1 | async-start | bytes 65536 | tf_op jit(solution)/shard_map/all_to_all | solution.py:26
  252.7 202.7 %reduce-scatter.2.cloned.1.call-start = ((), (), s32[]{:S(2)}) async-start(), calls=%async_computation.10 | async-start | bytes 9437184 | tf_op jit(solution)/shard_map/reduce_scatter | solution.py:101
  260.7 11.9 %copy-start.1 = (bf16[1024,1024]{0,1:T(8,128)(2,1)S(1)}, bf16[1024,1024]{0,1:T(8,128)(2,1)}, u32[]{:S(2)}) copy-start(bf16[1024,1024]{0,1:T(8,128)(2,1)} %copy.66) | copy-start | bytes 6291460
  288.0 0.8 copy-start.4
  288.0 1.0 copy-start.5
  289.1 7.1 %copy-start.2 = (bf16[1024,512]{1,0:T(8,128)(2,1)S(1)}, bf16[1024,512]{1,0:T(8,128)(2,1)}, u32[]{:S(2)}) copy-start(bf16[1024,512]{1,0:T(8,128)(2,1)} %param.16) | copy-start | bytes 3145732
  344.8 117.6 %all-to-all-start = ((f32[8,1,1024]{2,1,0:T(1,128)}), f32[8,1,1024]{2,1,0:T(1,128)S(1)}, u32[]{:S(2)}, u32[]{:S(2)}) async-start(f32[8,1,1024]{2,1,0:T(1,128)} %broadcast_in_dim.32), calls=%async_computation | async-start | bytes 65536 | tf_op jit(solution)/shard_map/all_to_all | solution.py:26
  461.1 7.2 %copy-start.7 = (bf16[512]{0:T(512)(128)(2,1)S(1)}, bf16[512]{0:T(512)(128)(2,1)}, u32[]{:S(2)}) copy-start(bf16[512]{0:T(512)(128)(2,1)} %param.19) | copy-start | bytes 3076
  462.3 22.8 %all-to-all-start.2 = ((bf16[16,64,513]{2,1,0:T(8,128)(2,1)}), bf16[16,64,513]{2,1,0:T(8,128)(2,1)S(1)}, u32[]{:S(2)}, u32[]{:S(2)}) async-start(bf16[16,64,513]{2,1,0:T(8,128)(2,1)} %pad_maximum_fusion), calls=%async_computation.3 | async-start | bytes 2621440 | tf_op jit(solution)/shard_map/all_to_all | solution.py:40
  502.4 14.7 %all-to-all-start.5 = ((f32[16,1,512]{2,1,0:T(1,128)}), f32[16,1,512]{2,1,0:T(1,128)S(1)}, u32[]{:S(2)}, u32[]{:S(2)}) async-start(f32[16,1,512]{2,1,0:T(1,128)} %broadcast_in_dim.63), calls=%async_computation.6 | async-start | bytes 65536 | tf_op jit(solution)/shard_map/all_to_all | solution.py:26
  517.1 34.1 %all-to-all-start.4 = ((bf16[16,128,512]{1,2,0:T(8,128)(2,1)}), bf16[16,128,512]{1,2,0:T(8,128)(2,1)S(1)}, u32[]{:S(2)}, u32[]{:S(2)}) async-start(bf16[16,128,512]{1,2,0:T(8,128)(2,1)} %bitcast.41), calls=%async_computation.5 | async-start | bytes 4194304 | tf_op jit(solution)/shard_map/all_to_all | solution.py:59
Sparse Core Ops, SparseCore 0:
  10.2 120.5 all-gather.9
  132.4 97.8 all-gather.7
  232.7 70.9 all-gather.11
  305.3 32.2 all-gather.5
  341.3 114.1 reduce-scatter.1
